TPU v7x, 32 devices: a whole 2x2x4 slice. The times are simulated.
32 devices in a mesh: head: 2 (over x), inner: 4 (over y, core), outer: 4 (over z).
Axes of the slice: x: 2, y: 2, z: 4, core: 2. Of those that a mesh axis runs over, the one named last changes fastest.
Arguments:
- queries: float32 [2048, 8, 128], P(('inner', 'outer'), 'head'), may hold values from -8 to 8
- key_rows: float32 [2048, 128], P(('inner', 'outer'), 'head'), may hold values from -8 to 8
- values: float32 [2048, 128], P(('inner', 'outer'), 'head'), may hold values from -24 to 24
- out_grad: float32 [2048, 8, 128], P(('inner', 'outer'), 'head'), may hold values from -48 to 48
- sink_len: int32 [1], replicated, may hold values from 32 to 128
- window_len: int32 [1], replicated, may hold values from 129 to 640
- block_codes: int32 [16, 5], replicated, may hold values from 0 to 2, as said below
Outputs:
- query_grad: float32 [2048, 8, 128], P(('inner', 'outer'), 'head')
- key_grad: float32 [2048, 128], P(('inner', 'outer'), 'head')
- value_grad: float32 [2048, 128], P(('inner', 'outer'), 'head')
Inputs may be any that keep to these rules, and one draw needn't show every extreme that they name: block_codes[b, 0] is 1 or 2 for every block b.
All inputs are finite; a program needn't handle non-finite values.
Results may differ from a plain program's by a relative error of at most 0.0003.
Values sent between devices are 32-bit elements; how exact they have to be, the bound alone decides.
A program may use at most 64 MiB of HBM per device.

v0:
```python
import math
import jax
import jax.numpy as jnp
from jax import lax
from jax.sharding import PartitionSpec as P

STEPS = 5
SINK = 128
very_low = -1e30
precise = lax.Precision.HIGHEST


def swapped(array, axis, distance):
    return lax.ppermute(array, axis, [(i, i ^ 1 << distance) for i in range(lax.axis_size(axis))])


def spread(array, axis, root):
    mine = lax.axis_index(axis) == root
    return lax.psum(jnp.where(mine, array, jnp.zeros_like(array)), axis)


def shifted(value, axis, steps):
    count = lax.axis_size(axis)
    pairs = [(source, (source + steps) % count) for source in range(count)]
    return lax.ppermute(value, axis, pairs)


def codes_for(block_codes, query_block, offset):
    row_ids = jnp.arange(block_codes.shape[0], dtype=jnp.int32)
    return jnp.sum(jnp.where(row_ids == query_block, block_codes[:, offset], 0))


def visible(query_block, key_block, offset, block_rows, sink_end, window, block_codes, present):
    local_ids = jnp.arange(block_rows, dtype=jnp.int32)
    pos_q = query_block * block_rows + local_ids
    pos_k = key_block * block_rows + local_ids
    code = codes_for(block_codes, query_block, offset)
    near = pos_q[:, None] - pos_k[None, :] < window
    rule = (code != 0) & ((code == 2) | near)
    in_sink = (pos_k < sink_end)[None, :]
    chosen = jnp.where(query_block == 0, in_sink | rule, jnp.logical_not(in_sink) & rule)
    return present & (pos_k[None, :] <= pos_q[:, None]) & chosen


def scores(query_blk, key_blk, temper):
    return temper * jnp.einsum("qhd,kd->hqk", query_blk, key_blk, precision=precise)


def forward_step(running, query_blk, key_blk, value_blk, allowed, temper):
    row_max, row_sum, carried = running
    logits = jnp.where(allowed[None], scores(query_blk, key_blk, temper), very_low)
    new_max = jnp.maximum(row_max, jnp.max(logits, axis=2))
    factor = jnp.exp(row_max - new_max)
    weights = jnp.where(allowed[None], jnp.exp(logits - new_max[:, :, None]), 0.0)
    row_sum = row_sum * factor + jnp.sum(weights, axis=2)
    carried = carried * factor[:, :, None] + jnp.einsum(
        "hqk,kd->hqd", weights, value_blk, precision=precise
    )
    return ((new_max, row_sum, carried), logits)


def finish(running, grad_blk):
    row_max, row_sum, carried = running
    log_sum = row_max + jnp.log(row_sum)
    row_delta = jnp.sum(jnp.transpose(grad_blk, (1, 0, 2)) * carried, axis=2) / row_sum
    return (log_sum, row_delta)


def backward_step(
    query_blk, grad_blk, log_sum, row_delta, key_blk, value_blk, allowed, temper, cached
):
    if cached is None:
        cached = scores(query_blk, key_blk, temper)
    weights = jnp.where(allowed[None], jnp.exp(cached - log_sum[:, :, None]), 0.0)
    grad_dots = jnp.einsum("qhd,kd->hqk", grad_blk, value_blk, precision=precise)
    dscores = weights * (grad_dots - row_delta[:, :, None])
    step_dq = temper * jnp.einsum("hqk,kd->qhd", dscores, key_blk, precision=precise)
    step_dk = temper * jnp.einsum("hqk,qhd->kd", dscores, query_blk, precision=precise)
    step_dv = jnp.einsum("hqk,qhd->kd", weights, grad_blk, precision=precise)
    return (step_dq, step_dk, step_dv)


def shards(queries, key_rows, values, out_grad, sink_len, window_len, block_codes):
    block_rows, heads_dev, head_dim = queries.shape
    temper = 1.0 / math.sqrt(head_dim)
    sink_end = sink_len[0]
    window = window_len[0]
    seq_index = lax.axis_index(("inner", "outer"))
    seq_count = lax.axis_size(("inner", "outer"))
    upper_half = lax.axis_index("head") % 2 == 1
    other_keys, other_values = swapped((key_rows, values), "head", 0)
    key_full = jnp.where(
        upper_half,
        jnp.concatenate([other_keys, key_rows], 1),
        jnp.concatenate([key_rows, other_keys], 1),
    )
    value_full = jnp.where(
        upper_half,
        jnp.concatenate([other_values, values], 1),
        jnp.concatenate([values, other_values], 1),
    )
    sink_keys, sink_values = (
        spread(key_full, ("inner", "outer"), 0),
        spread(value_full, ("inner", "outer"), 0),
    )
    sink_ids = jnp.arange(SINK, dtype=jnp.int32)
    sink_allowed = jnp.broadcast_to(
        ((seq_index >= 1) & (sink_ids < sink_end))[None, :], (block_rows, SINK)
    )
    carried = jnp.zeros((heads_dev, block_rows, head_dim), jnp.float32)
    running = (
        jnp.full((heads_dev, block_rows), very_low, jnp.float32),
        jnp.zeros((heads_dev, block_rows), jnp.float32),
        carried,
    )
    running, ignored = forward_step(running, queries, sink_keys, sink_values, sink_allowed, temper)
    grad_keys = jnp.zeros((block_rows, head_dim), jnp.float32)
    grad_values = jnp.zeros((block_rows, head_dim), jnp.float32)
    moving_k, moving_v = (key_full, value_full)
    cached = None
    for offset in range(STEPS):
        if offset > 0:
            moving_k, moving_v = shifted((moving_k, moving_v), ("inner", "outer"), 1)
        allowed = visible(
            seq_index,
            (seq_index - offset) % seq_count,
            offset,
            block_rows,
            sink_end,
            window,
            block_codes,
            seq_index - offset >= 0,
        )
        running, cached = forward_step(running, queries, moving_k, moving_v, allowed, temper)
    log_sum, row_delta = finish(running, out_grad)
    grad_q = jnp.zeros_like(queries)
    for offset in range(STEPS - 1, -1, -1):
        if offset < STEPS - 1:
            moving_k, moving_v, grad_keys, grad_values = shifted(
                (moving_k, moving_v, grad_keys, grad_values), ("inner", "outer"), -1
            )
            cached = None
        allowed = visible(
            seq_index,
            (seq_index - offset) % seq_count,
            offset,
            block_rows,
            sink_end,
            window,
            block_codes,
            seq_index - offset >= 0,
        )
        step_dq, step_dk, step_dv = backward_step(
            queries, out_grad, log_sum, row_delta, moving_k, moving_v, allowed, temper, cached
        )
        grad_q = grad_q + step_dq
        grad_keys = grad_keys + step_dk
        grad_values = grad_values + step_dv
    sink_dq, sink_dk, sink_dv = backward_step(
        queries, out_grad, log_sum, row_delta, sink_keys, sink_values, sink_allowed, temper, None
    )
    grad_q = grad_q + sink_dq
    total_dk, total_dv = lax.psum((sink_dk, sink_dv), ("inner", "outer"))
    is_first = seq_index == 0
    grad_keys = grad_keys.at[:SINK].add(jnp.where(is_first, total_dk, 0.0))
    grad_values = grad_values.at[:SINK].add(jnp.where(is_first, total_dv, 0.0))
    half_cols = key_rows.shape[1]
    keep_k = jnp.where(upper_half, grad_keys[:, half_cols:], grad_keys[:, :half_cols])
    send_k = jnp.where(upper_half, grad_keys[:, :half_cols], grad_keys[:, half_cols:])
    keep_v = jnp.where(upper_half, grad_values[:, half_cols:], grad_values[:, :half_cols])
    send_v = jnp.where(upper_half, grad_values[:, :half_cols], grad_values[:, half_cols:])
    got_k, got_v = swapped((send_k, send_v), "head", 0)
    return (grad_q, keep_k + got_k, keep_v + got_v)


def solution(mesh):
    in_specs = (
        P(("inner", "outer"), "head", None),
        P(("inner", "outer"), "head"),
        P(("inner", "outer"), "head"),
        P(("inner", "outer"), "head", None),
        P(),
        P(),
        P(),
    )
    out_specs = (
        P(("inner", "outer"), "head", None),
        P(("inner", "outer"), "head"),
        P(("inner", "outer"), "head"),
    )
    return jax.shard_map(shards, mesh=mesh, in_specs=in_specs, out_specs=out_specs, check_vma=False)
```

profile of v0, /device:TPU:8, one launch (start us, length us, event | category | flops | bytes accessed | tf_op | source)
XLA Modules:
  0.0 250.2 jit_solution(6072486249846511252)
XLA Ops:
  7.2 0.9 copy.10
  8.1 1.6 collective-permute-start
  9.8 0.6 collective-permute-start.5
  10.4 0.7 copy-done.6
  11.1 0.7 fusion.159
  20.8 0.7 broadcast_select_fusion.1
  21.6 1.6 collective-permute-start.1
  23.2 0.7 broadcast_select_fusion
  23.9 1.6 collective-permute-start.6
  25.5 0.4 fusion.181
  26.2 1.6 collective-permute-start.2
  27.8 0.4 fusion.180
  28.2 88.4 %all-reduce.7.cloned.1.call-done = (f32[128,128]{1,0:T(8,128)}, f32[128,128]{1,0:T(8,128)}) async-done(((f32[128,128]{1,0:T(8,128)}, f32[128,128]{1,0:T(8,128)}), (f32[128,128]{1,0:T(8,128)}, f32[128,128]{1,0:T(8,128)})) %all-reduce.7.cloned.1.call-update) | async-done | bytes 131088 | tf_op jit(solution)/shard_map/psum | solution.py:19
  116.6 1.2 select_reduce_fusion
  117.9 2.0 collective-permute-start.3
  119.9 0.4 fusion.179
  120.3 1.8 collective-permute-done.7
  122.2 0.7 collective-permute-done.3
  122.9 1.3 collective-permute-start.4
  124.6 1.8 collective-permute-done.8
  126.4 0.7 collective-permute-start.9
  127.2 1.4 collective-permute-done.4
  128.6 0.4 fusion.177
  129.5 0.4 convolution_bitcast_fusion.11
  130.0 0.4 copy-done.3
  130.4 0.5 fusion.20
  130.9 0.4 fusion.19
  131.3 0.4 fusion.18
  131.8 0.4 fusion.17
  132.2 0.4 fusion.16
  132.7 1.1 convolution_bitcast_fusion.6
  133.7 0.4 fusion.48
  134.6 1.0 fusion.49
  135.6 0.4 fusion.123
  136.0 4.2 %collective-permute-start.23 = (f32[128,128]{1,0:T(8,128)S(1)}, f32[128,128]{1,0:T(8,128)S(1)}, u32[]{:S(2)}, u32[]{:S(2)}) collective-permute-start(f32[128,128]{1,0:T(8,128)S(1)} %convolution_bitcast_fusion.11), channel_id=1, source_target_pairs={{0,15},{1,0},{2,1},{3,2},{4,3},{5,4},{6,5},{7,6},{8,7},{9,8},{10,9... | collective-permute-start | bytes 196616 | tf_op jit(solution)/shard_map/ppermute | solution.py:25
  141.0 1.1 collective-permute-start.18
  142.3 0.4 fusion.127
  142.7 3.8 %collective-permute-done.10 = f32[128,128]{1,0:T(8,128)S(1)} collective-permute-done((f32[128,128]{1,0:T(8,128)S(1)}, f32[128,128]{1,0:T(8,128)S(1)}, u32[]{:S(2)}, u32[]{:S(2)}) %collective-permute-start.10) | collective-permute-done | bytes 65568 | tf_op jit(solution)/shard_map/ppermute | solution.py:25
  146.5 0.4 fusion.32
  147.3 1.3 collective-permute-start.24
  149.4 2.3 collective-permute-start.19
  151.8 0.4 convolution_add_fusion.3
  152.3 4.2 %collective-permute-done.12 = f32[128,128]{1,0:T(8,128)S(1)} collective-permute-done((f32[128,128]{1,0:T(8,128)S(1)}, f32[128,128]{1,0:T(8,128)S(1)}, u32[]{:S(2)}, u32[]{:S(2)}) %collective-permute-start.12) | collective-permute-done | bytes 65568 | tf_op jit(solution)/shard_map/ppermute | solution.py:25
  156.5 0.4 fusion.33
  157.3 1.8 collective-permute-start.25
  159.9 1.9 collective-permute-start.20
  161.9 0.5 collective-permute-start.14
  162.5 0.4 convolution_add_fusion.2
  162.9 3.8 %collective-permute-done.14 = f32[128,128]{1,0:T(8,128)S(1)} collective-permute-done((f32[128,128]{1,0:T(8,128)S(1)}, f32[128,128]{1,0:T(8,128)S(1)}, u32[]{:S(2)}, u32[]{:S(2)}) %collective-permute-start.14) | collective-permute-done | bytes 65568 | tf_op jit(solution)/shard_map/ppermute | solution.py:25
  166.8 0.4 fusion.34
  167.6 1.7 collective-permute-start.26
  170.1 2.8 %collective-permute-start.21 = (f32[128,128]{1,0:T(8,128)S(1)}, f32[128,128]{1,0:T(8,128)S(1)}, u32[]{:S(2)}, u32[]{:S(2)}) collective-permute-start(f32[128,128]{1,0:T(8,128)S(1)} %add.352), channel_id=1, source_target_pairs={{0,15},{1,0},{2,1},{3,2},{4,3},{5,4},{6,5},{7,6},{8,7},{9,8},{10,9... | collective-permute-start | bytes 196616 | tf_op jit(solution)/shard_map/ppermute | solution.py:25
  173.2 0.4 convolution_add_fusion.1
  173.6 3.6 %collective-permute-done.16 = f32[128,128]{1,0:T(8,128)S(1)} collective-permute-done((f32[128,128]{1,0:T(8,128)S(1)}, f32[128,128]{1,0:T(8,128)S(1)}, u32[]{:S(2)}, u32[]{:S(2)}) %collective-permute-start.16) | collective-permute-done | bytes 65568 | tf_op jit(solution)/shard_map/ppermute | solution.py:25
  177.1 0.4 fusion.35
  177.9 57.4 %all-reduce.5.cloned.1.call-done = (f32[128,128]{1,0:T(8,128)}, f32[128,128]{1,0:T(8,128)}) async-done(((f32[128,128]{1,0:T(8,128)}, f32[128,128]{1,0:T(8,128)}), (f32[128,128]{1,0:T(8,128)}, f32[128,128]{1,0:T(8,128)})) %all-reduce.5.cloned.1.call-update) | async-done | bytes 131088 | tf_op jit(solution)/shard_map/psum | solution.py:163
  235.4 1.5 collective-permute-start.27
  237.8 0.4 copy-done.4
  238.3 0.6 collective-permute-start.22
  238.9 0.4 fusion.2
  239.4 0.8 copy.78
  240.3 0.7 copy.80
  241.0 1.6 collective-permute-done.22
  242.7 0.7 copy.79
  (96 shorter events, 9.5 us)
Async XLA Ops:
  7.2 18.3 %copy-start = (f32[128,4,128]{2,1,0:T(4,128)S(1)}, f32[128,4,128]{2,1,0:T(4,128)}, u32[]{:S(2)}) copy-start(f32[128,4,128]{2,1,0:T(4,128)} %param.15) | copy-start | bytes 786436
  7.2 2.5 copy-start.5
  7.2 109.4 %all-reduce.7.cloned.1.call-start = ((), (), s32[]{:S(2)}) async-start(), calls=%async_computation.1 | async-start | bytes 262144 | tf_op jit(solution)/shard_map/psum | solution.py:19
  8.1 12.7 %collective-permute-start = (f32[128,64]{1,0:T(8,128)S(1)}, f32[128,64]{1,0:T(8,128)S(1)}, u32[]{:S(2)}, u32[]{:S(2)}) collective-permute-start(f32[128,64]{1,0:T(8,128)S(1)} %copy.10), channel_id=1, source_target_pairs={{0,16},{16,0},{1,17},{17,1},{2,18},{18,2},{3,19},{19,3},{4,20},{20... | collective-permute-start | bytes 98312 | tf_op jit(solution)/shard_map/ppermute | solution.py:14
  9.8 13.4 %collective-permute-start.5 = (f32[128,64]{1,0:T(8,128)S(1)}, f32[128,64]{1,0:T(8,128)S(1)}, u32[]{:S(2)}, u32[]{:S(2)}) collective-permute-start(f32[128,64]{1,0:T(8,128)S(1)} %copy.24), channel_id=1, source_target_pairs={{0,16},{16,0},{1,17},{17,1},{2,18},{18,2},{3,19},{19,3},{4,20},{20... | collective-permute-start | bytes 98312 | tf_op jit(solution)/shard_map/ppermute | solution.py:14
  10.4 0.7 copy-start.6
  10.4 10.3 %copy-start.1 = (f32[128,4,128]{2,1,0:T(4,128)S(1)}, f32[128,4,128]{2,1,0:T(4,128)}, u32[]{:S(2)}) copy-start(f32[128,4,128]{2,1,0:T(4,128)} %param.18) | copy-start | bytes 786436
  21.6 4.6 %collective-permute-start.1 = (f32[128,128]{1,0:T(8,128)S(1)}, f32[128,128]{1,0:T(8,128)S(1)}, u32[]{:S(2)}, u32[]{:S(2)}) collective-permute-start(f32[128,128]{1,0:T(8,128)S(1)} %get-tuple-element.80), channel_id=1, source_target_pairs={{0,1},{1,2},{2,3},{3,4},{4,5},{5,6},{6,7},{7,8},{8,9},{9,10},{10,1... | collective-permute-start | bytes 196616 | tf_op jit(solution)/shard_map/ppermute | solution.py:25
  23.9 94.0 %collective-permute-start.6 = (f32[128,128]{1,0:T(8,128)S(1)}, f32[128,128]{1,0:T(8,128)S(1)}, u32[]{:S(2)}, u32[]{:S(2)}) collective-permute-start(f32[128,128]{1,0:T(8,128)S(1)} %get-tuple-element.78), channel_id=1, source_target_pairs={{0,1},{1,2},{2,3},{3,4},{4,5},{5,6},{6,7},{7,8},{8,9},{9,10},{10,1... | collective-permute-start | bytes 196616 | tf_op jit(solution)/shard_map/ppermute | solution.py:25
  25.9 209.4 %all-reduce.5.cloned.1.call-start = ((), (), s32[]{:S(2)}) async-start(), calls=%async_computation | async-start | bytes 262144 | tf_op jit(solution)/shard_map/psum | solution.py:163
  26.2 91.7 %collective-permute-start.2 = (f32[128,128]{1,0:T(8,128)S(1)}, f32[128,128]{1,0:T(8,128)S(1)}, u32[]{:S(2)}, u32[]{:S(2)}) collective-permute-start(f32[128,128]{1,0:T(8,128)S(1)} %collective-permute-done.1), channel_id=1, source_target_pairs={{0,1},{1,2},{2,3},{3,4},{4,5},{5,6},{6,7},{7,8},{8,9},{9,10},{10,1... | collective-permute-start | bytes 196616 | tf_op jit(solution)/shard_map/ppermute | solution.py:25
  117.8 4.3 %collective-permute-start.7 = (f32[128,128]{1,0:T(8,128)S(1)}, f32[128,128]{1,0:T(8,128)S(1)}, u32[]{:S(2)}, u32[]{:S(2)}) collective-permute-start(f32[128,128]{1,0:T(8,128)S(1)} %collective-permute-done.6), channel_id=1, source_target_pairs={{0,1},{1,2},{2,3},{3,4},{4,5},{5,6},{6,7},{7,8},{8,9},{9,10},{10,1... | collective-permute-start | bytes 196616 | tf_op jit(solution)/shard_map/ppermute | solution.py:25
  117.9 4.9 %collective-permute-start.3 = (f32[128,128]{1,0:T(8,128)S(1)}, f32[128,128]{1,0:T(8,128)S(1)}, u32[]{:S(2)}, u32[]{:S(2)}) collective-permute-start(f32[128,128]{1,0:T(8,128)S(1)} %collective-permute-done.2), channel_id=1, source_target_pairs={{0,1},{1,2},{2,3},{3,4},{4,5},{5,6},{6,7},{7,8},{8,9},{9,10},{10,1... | collective-permute-start | bytes 196616 | tf_op jit(solution)/shard_map/ppermute | solution.py:25
  122.2 4.3 %collective-permute-start.8 = (f32[128,128]{1,0:T(8,128)S(1)}, f32[128,128]{1,0:T(8,128)S(1)}, u32[]{:S(2)}, u32[]{:S(2)}) collective-permute-start(f32[128,128]{1,0:T(8,128)S(1)} %collective-permute-done.7), channel_id=1, source_target_pairs={{0,1},{1,2},{2,3},{3,4},{4,5},{5,6},{6,7},{7,8},{8,9},{9,10},{10,1... | collective-permute-start | bytes 196616 | tf_op jit(solution)/shard_map/ppermute | solution.py:25
  122.9 5.7 %collective-permute-start.4 = (f32[128,128]{1,0:T(8,128)S(1)}, f32[128,128]{1,0:T(8,128)S(1)}, u32[]{:S(2)}, u32[]{:S(2)}) collective-permute-start(f32[128,128]{1,0:T(8,128)S(1)} %collective-permute-done.3), channel_id=1, source_target_pairs={{0,1},{1,2},{2,3},{3,4},{4,5},{5,6},{6,7},{7,8},{8,9},{9,10},{10,1... | collective-permute-start | bytes 196616 | tf_op jit(solution)/shard_map/ppermute | solution.py:25
  126.4 7.3 %collective-permute-start.9 = (f32[128,128]{1,0:T(8,128)S(1)}, f32[128,128]{1,0:T(8,128)S(1)}, u32[]{:S(2)}, u32[]{:S(2)}) collective-permute-start(f32[128,128]{1,0:T(8,128)S(1)} %collective-permute-done.8), channel_id=1, source_target_pairs={{0,1},{1,2},{2,3},{3,4},{4,5},{5,6},{6,7},{7,8},{8,9},{9,10},{10,1... | collective-permute-start | bytes 196616 | tf_op jit(solution)/shard_map/ppermute | solution.py:25
  129.5 0.8 copy-start.3
  134.6 1.0 copy-start.2
  136.0 10.9 %collective-permute-start.23 = (f32[128,128]{1,0:T(8,128)S(1)}, f32[128,128]{1,0:T(8,128)S(1)}, u32[]{:S(2)}, u32[]{:S(2)}) collective-permute-start(f32[128,128]{1,0:T(8,128)S(1)} %convolution_bitcast_fusion.11), channel_id=1, source_target_pairs={{0,15},{1,0},{2,1},{3,2},{4,3},{5,4},{6,5},{7,6},{8,7},{9,8},{10,9... | collective-permute-start | bytes 196616 | tf_op jit(solution)/shard_map/ppermute | solution.py:25
  141.0 8.0 %collective-permute-start.18 = (f32[128,128]{1,0:T(8,128)S(1)}, f32[128,128]{1,0:T(8,128)S(1)}, u32[]{:S(2)}, u32[]{:S(2)}) collective-permute-start(f32[128,128]{1,0:T(8,128)S(1)} %fusion.54), channel_id=1, source_target_pairs={{0,15},{1,0},{2,1},{3,2},{4,3},{5,4},{6,5},{7,6},{8,7},{9,8},{10,9... | collective-permute-start | bytes 196616 | tf_op jit(solution)/shard_map/ppermute | solution.py:25
  142.2 4.3 %collective-permute-start.10 = (f32[128,128]{1,0:T(8,128)S(1)}, f32[128,128]{1,0:T(8,128)S(1)}, u32[]{:S(2)}, u32[]{:S(2)}) collective-permute-start(f32[128,128]{1,0:T(8,128)S(1)} %collective-permute-done.4), channel_id=1, source_target_pairs={{0,15},{1,0},{2,1},{3,2},{4,3},{5,4},{6,5},{7,6},{8,7},{9,8},{10,9... | collective-permute-start | bytes 196616 | tf_op jit(solution)/shard_map/ppermute | solution.py:25
  142.2 6.4 %collective-permute-start.11 = (f32[128,128]{1,0:T(8,128)S(1)}, f32[128,128]{1,0:T(8,128)S(1)}, u32[]{:S(2)}, u32[]{:S(2)}) collective-permute-start(f32[128,128]{1,0:T(8,128)S(1)} %collective-permute-done.9), channel_id=1, source_target_pairs={{0,15},{1,0},{2,1},{3,2},{4,3},{5,4},{6,5},{7,6},{8,7},{9,8},{10,9... | collective-permute-start | bytes 196616 | tf_op jit(solution)/shard_map/ppermute | solution.py:25
  147.3 10.0 %collective-permute-start.24 = (f32[128,128]{1,0:T(8,128)S(1)}, f32[128,128]{1,0:T(8,128)S(1)}, u32[]{:S(2)}, u32[]{:S(2)}) collective-permute-start(f32[128,128]{1,0:T(8,128)S(1)} %fusion.56), channel_id=1, source_target_pairs={{0,15},{1,0},{2,1},{3,2},{4,3},{5,4},{6,5},{7,6},{8,7},{9,8},{10,9... | collective-permute-start | bytes 196616 | tf_op jit(solution)/shard_map/ppermute | solution.py:25
  149.4 10.5 %collective-permute-start.19 = (f32[128,128]{1,0:T(8,128)S(1)}, f32[128,128]{1,0:T(8,128)S(1)}, u32[]{:S(2)}, u32[]{:S(2)}) collective-permute-start(f32[128,128]{1,0:T(8,128)S(1)} %fusion.55), channel_id=1, source_target_pairs={{0,15},{1,0},{2,1},{3,2},{4,3},{5,4},{6,5},{7,6},{8,7},{9,8},{10,9... | collective-permute-start | bytes 196616 | tf_op jit(solution)/shard_map/ppermute | solution.py:25
  151.7 4.8 %collective-permute-start.12 = (f32[128,128]{1,0:T(8,128)S(1)}, f32[128,128]{1,0:T(8,128)S(1)}, u32[]{:S(2)}, u32[]{:S(2)}) collective-permute-start(f32[128,128]{1,0:T(8,128)S(1)} %collective-permute-done.10), channel_id=1, source_target_pairs={{0,15},{1,0},{2,1},{3,2},{4,3},{5,4},{6,5},{7,6},{8,7},{9,8},{10,9... | collective-permute-start | bytes 196616 | tf_op jit(solution)/shard_map/ppermute | solution.py:25
  151.8 7.4 %collective-permute-start.13 = (f32[128,128]{1,0:T(8,128)S(1)}, f32[128,128]{1,0:T(8,128)S(1)}, u32[]{:S(2)}, u32[]{:S(2)}) collective-permute-start(f32[128,128]{1,0:T(8,128)S(1)} %collective-permute-done.11), channel_id=1, source_target_pairs={{0,15},{1,0},{2,1},{3,2},{4,3},{5,4},{6,5},{7,6},{8,7},{9,8},{10,9... | collective-permute-start | bytes 196616 | tf_op jit(solution)/shard_map/ppermute | solution.py:25
  157.3 10.2 %collective-permute-start.25 = (f32[128,128]{1,0:T(8,128)S(1)}, f32[128,128]{1,0:T(8,128)S(1)}, u32[]{:S(2)}, u32[]{:S(2)}) collective-permute-start(f32[128,128]{1,0:T(8,128)S(1)} %add.357), channel_id=1, source_target_pairs={{0,15},{1,0},{2,1},{3,2},{4,3},{5,4},{6,5},{7,6},{8,7},{9,8},{10,9... | collective-permute-start | bytes 196616 | tf_op jit(solution)/shard_map/ppermute | solution.py:25
  159.9 10.1 %collective-permute-start.20 = (f32[128,128]{1,0:T(8,128)S(1)}, f32[128,128]{1,0:T(8,128)S(1)}, u32[]{:S(2)}, u32[]{:S(2)}) collective-permute-start(f32[128,128]{1,0:T(8,128)S(1)} %add.351), channel_id=1, source_target_pairs={{0,15},{1,0},{2,1},{3,2},{4,3},{5,4},{6,5},{7,6},{8,7},{9,8},{10,9... | collective-permute-start | bytes 196616 | tf_op jit(solution)/shard_map/ppermute | solution.py:25
  161.9 4.9 %collective-permute-start.14 = (f32[128,128]{1,0:T(8,128)S(1)}, f32[128,128]{1,0:T(8,128)S(1)}, u32[]{:S(2)}, u32[]{:S(2)}) collective-permute-start(f32[128,128]{1,0:T(8,128)S(1)} %collective-permute-done.12), channel_id=1, source_target_pairs={{0,15},{1,0},{2,1},{3,2},{4,3},{5,4},{6,5},{7,6},{8,7},{9,8},{10,9... | collective-permute-start | bytes 196616 | tf_op jit(solution)/shard_map/ppermute | solution.py:25
  162.4 6.8 %collective-permute-start.15 = (f32[128,128]{1,0:T(8,128)S(1)}, f32[128,128]{1,0:T(8,128)S(1)}, u32[]{:S(2)}, u32[]{:S(2)}) collective-permute-start(f32[128,128]{1,0:T(8,128)S(1)} %collective-permute-done.13), channel_id=1, source_target_pairs={{0,15},{1,0},{2,1},{3,2},{4,3},{5,4},{6,5},{7,6},{8,7},{9,8},{10,9... | collective-permute-start | bytes 196616 | tf_op jit(solution)/shard_map/ppermute | solution.py:25
  167.6 67.7 %collective-permute-start.26 = (f32[128,128]{1,0:T(8,128)S(1)}, f32[128,128]{1,0:T(8,128)S(1)}, u32[]{:S(2)}, u32[]{:S(2)}) collective-permute-start(f32[128,128]{1,0:T(8,128)S(1)} %add.358), channel_id=1, source_target_pairs={{0,15},{1,0},{2,1},{3,2},{4,3},{5,4},{6,5},{7,6},{8,7},{9,8},{10,9... | collective-permute-start | bytes 196616 | tf_op jit(solution)/shard_map/ppermute | solution.py:25
  170.1 67.7 %collective-permute-start.21 = (f32[128,128]{1,0:T(8,128)S(1)}, f32[128,128]{1,0:T(8,128)S(1)}, u32[]{:S(2)}, u32[]{:S(2)}) collective-permute-start(f32[128,128]{1,0:T(8,128)S(1)} %add.352), channel_id=1, source_target_pairs={{0,15},{1,0},{2,1},{3,2},{4,3},{5,4},{6,5},{7,6},{8,7},{9,8},{10,9... | collective-permute-start | bytes 196616 | tf_op jit(solution)/shard_map/ppermute | solution.py:25
  172.9 4.3 %collective-permute-start.16 = (f32[128,128]{1,0:T(8,128)S(1)}, f32[128,128]{1,0:T(8,128)S(1)}, u32[]{:S(2)}, u32[]{:S(2)}) collective-permute-start(f32[128,128]{1,0:T(8,128)S(1)} %collective-permute-done.14), channel_id=1, source_target_pairs={{0,15},{1,0},{2,1},{3,2},{4,3},{5,4},{6,5},{7,6},{8,7},{9,8},{10,9... | collective-permute-start | bytes 196616 | tf_op jit(solution)/shard_map/ppermute | solution.py:25
  173.1 63.9 %collective-permute-start.17 = (f32[128,128]{1,0:T(8,128)S(1)}, f32[128,128]{1,0:T(8,128)S(1)}, u32[]{:S(2)}, u32[]{:S(2)}) collective-permute-start(f32[128,128]{1,0:T(8,128)S(1)} %collective-permute-done.15), channel_id=1, source_target_pairs={{0,15},{1,0},{2,1},{3,2},{4,3},{5,4},{6,5},{7,6},{8,7},{9,8},{10,9... | collective-permute-start | bytes 196616 | tf_op jit(solution)/shard_map/ppermute | solution.py:25
  235.4 4.8 %collective-permute-start.27 = (f32[128,64]{1,0:T(8,128)S(1)}, f32[128,64]{1,0:T(8,128)S(1)}, u32[]{:S(2)}, u32[]{:S(2)}) collective-permute-start(f32[128,64]{1,0:T(8,128)S(1)} %slice_select_fusion), channel_id=1, source_target_pairs={{0,16},{16,0},{1,17},{17,1},{2,18},{18,2},{3,19},{19,3},{4,20},{20... | collective-permute-start | bytes 98312 | tf_op jit(solution)/shard_map/ppermute | solution.py:14
  237.3 0.8 copy-start.4
  238.3 4.3 %collective-permute-start.22 = (f32[128,64]{1,0:T(8,128)S(1)}, f32[128,64]{1,0:T(8,128)S(1)}, u32[]{:S(2)}, u32[]{:S(2)}) collective-permute-start(f32[128,64]{1,0:T(8,128)S(1)} %slice_select_fusion.1), channel_id=1, source_target_pairs={{0,16},{16,0},{1,17},{17,1},{2,18},{18,2},{3,19},{19,3},{4,20},{20... | collective-permute-start | bytes 98312 | tf_op jit(solution)/shard_map/ppermute | solution.py:14
Sparse Core Ops, SparseCore 0:
  26.0 90.5 all-reduce.6
  142.3 92.9 all-reduce.4
where the time goes:
time: 251 us; the launch traced here: 250 us
  waiting for transfers between devices  169 us (67%)
  starting transfers between devices  31.6 us (13%)
  between operations  22.4 us (9%)
  matrix products  18.4 us (7%)
  local copies, waits for them, and re-layouts  5.47 us (2%)
  other arithmetic  3.54 us (1%)
    psum x1, waiting for transfers between devices, spread(): return lax.psum(jnp.where(mine, array, jnp.zeros_like(array)), axis)  88.4 us
    psum x1, waiting for transfers between devices, shards(): total_dk, total_dv = lax.psum((sink_dk, sink_dv), ('inner', 'outer'))  57.4 us
    ppermute x24, starting transfers between devices, shifted(): return lax.ppermute(value, axis, pairs)  27.2 us
    ppermute x24, waiting for transfers between devices, shifted(): return lax.ppermute(value, axis, pairs)  21.4 us
  transfers between devices with their start and end apart: 30, of which 12 were waited for; matrix products, arithmetic and copies ran while one was open for 9% of the time, Pallas kernels for 0%

commit v1 on v0

--- a/solution.py
+++ b/solution.py
@@ -160,7 +160,7 @@
         queries, out_grad, log_sum, row_delta, sink_keys, sink_values, sink_allowed, temper, None
     )
     grad_q = grad_q + sink_dq
-    total_dk, total_dv = lax.psum((sink_dk, sink_dv), ("inner", "outer"))
+    total_dk, total_dv = lax.psum(lax.psum((sink_dk, sink_dv), "outer"), "inner")
     is_first = seq_index == 0
     grad_keys = grad_keys.at[:SINK].add(jnp.where(is_first, total_dk, 0.0))
     grad_values = grad_values.at[:SINK].add(jnp.where(is_first, total_dv, 0.0))

time: 251 us -> 229 us (0.912); the launches traced: 250 us -> 226 us
  waiting for transfers between devices: 169 us -> 144 us
    psum x1 -> x2, waiting for transfers between devices: 57.4 us -> 34.1 us  [the longest x1 19.4 us: shards(): lax.psum(lax.psum((sink_dk, sink_dv), 'outer'), 'inner')]
  transfers between devices with their start and end apart: 30 -> 31, of which waited for: 12 -> 13; matrix products, arithmetic and copies ran while one was open for 9% -> 10% of each run, Pallas kernels for 0% -> 0%
where the time goes in v1:
time: 229 us; the launch traced here: 226 us
  waiting for transfers between devices  144 us (63%)
  starting transfers between devices  31.9 us (14%)
  between operations  22.2 us (10%)
  matrix products  18.4 us (8%)
  local copies, waits for them, and re-layouts  5.47 us (2%)
  other arithmetic  3.62 us (2%)
    psum x1, waiting for transfers between devices, spread(): return lax.psum(jnp.where(mine, array, jnp.zeros_like(array)), axis)  88.4 us
    ppermute x24, starting transfers between devices, shifted(): return lax.ppermute(value, axis, pairs)  27.4 us
    ppermute x24, waiting for transfers between devices, shifted(): return lax.ppermute(value, axis, pairs)  20 us
    psum x1, waiting for transfers between devices, shards(): lax.psum(lax.psum((sink_dk, sink_dv), 'outer'), 'inner')  19.4 us
    psum x1, waiting for transfers between devices, shards(): lax.psum((sink_dk, sink_dv), 'outer')  14.7 us
    dot_general x10, matrix products, scores(): jnp.einsum('qhd,kd->hqk', query_blk, key_blk, precision=precise)  4.88 us
    unnamed x20, local copies, waits for them, and re-layouts  4.87 us
  transfers between devices with their start and end apart: 31, of which 13 were waited for; matrix products, arithmetic and copies ran while one was open for 10% of the time, Pallas kernels for 0%

profile of v1, /device:TPU:8, one launch (start us, length us, event | category | flops | bytes accessed | tf_op | source)
XLA Modules:
  0.0 225.7 jit_solution(6699235813355351526)
XLA Ops:
  7.2 0.9 copy.10
  8.1 1.6 collective-permute-start
  9.8 0.6 collective-permute-start.5
  10.4 0.7 copy-done.6
  11.1 0.8 fusion.159
  20.9 0.7 broadcast_select_fusion.1
  21.7 1.6 collective-permute-start.1
  23.3 0.7 broadcast_select_fusion
  24.0 1.6 collective-permute-start.6
  25.6 0.4 fusion.181
  26.3 1.6 collective-permute-start.2
  28.3 88.4 %all-reduce.7.cloned.1.call-done = (f32[128,128]{1,0:T(8,128)}, f32[128,128]{1,0:T(8,128)}) async-done(((f32[128,128]{1,0:T(8,128)}, f32[128,128]{1,0:T(8,128)}), (f32[128,128]{1,0:T(8,128)}, f32[128,128]{1,0:T(8,128)})) %all-reduce.7.cloned.1.call-update) | async-done | bytes 131088 | tf_op jit(solution)/shard_map/psum | solution.py:19
  116.7 1.2 select_reduce_fusion
  118.1 2.0 collective-permute-start.3
  120.1 0.4 fusion.179
  120.5 1.8 collective-permute-done.7
  122.4 0.7 collective-permute-done.3
  123.0 1.3 collective-permute-start.4
  124.7 1.9 collective-permute-done.8
  126.6 0.7 collective-permute-start.9
  127.3 1.4 collective-permute-done.4
  129.7 0.4 convolution_bitcast_fusion.11
  130.5 0.5 fusion.20
  131.0 0.4 fusion.19
  131.5 0.4 fusion.18
  131.9 0.4 fusion.17
  132.4 0.4 fusion.16
  132.8 1.1 convolution_bitcast_fusion.6
  133.9 0.4 fusion.48
  134.7 1.0 fusion.49
  135.8 0.4 fusion.123
  136.2 4.2 %collective-permute-start.23 = (f32[128,128]{1,0:T(8,128)S(1)}, f32[128,128]{1,0:T(8,128)S(1)}, u32[]{:S(2)}, u32[]{:S(2)}) collective-permute-start(f32[128,128]{1,0:T(8,128)S(1)} %convolution_bitcast_fusion.11), channel_id=1, source_target_pairs={{0,15},{1,0},{2,1},{3,2},{4,3},{5,4},{6,5},{7,6},{8,7},{9,8},{10,9... | collective-permute-start | bytes 196616 | tf_op jit(solution)/shard_map/ppermute | solution.py:25
  141.2 1.1 collective-permute-start.18
  142.5 0.4 fusion.127
  143.0 3.8 %collective-permute-done.10 = f32[128,128]{1,0:T(8,128)S(1)} collective-permute-done((f32[128,128]{1,0:T(8,128)S(1)}, f32[128,128]{1,0:T(8,128)S(1)}, u32[]{:S(2)}, u32[]{:S(2)}) %collective-permute-start.10) | collective-permute-done | bytes 65568 | tf_op jit(solution)/shard_map/ppermute | solution.py:25
  146.7 0.4 fusion.32
  147.5 1.2 collective-permute-start.24
  149.5 2.3 %collective-permute-start.19 = (f32[128,128]{1,0:T(8,128)S(1)}, f32[128,128]{1,0:T(8,128)S(1)}, u32[]{:S(2)}, u32[]{:S(2)}) collective-permute-start(f32[128,128]{1,0:T(8,128)S(1)} %fusion.55), channel_id=1, source_target_pairs={{0,15},{1,0},{2,1},{3,2},{4,3},{5,4},{6,5},{7,6},{8,7},{9,8},{10,9... | collective-permute-start | bytes 196616 | tf_op jit(solution)/shard_map/ppermute | solution.py:25
  152.0 0.4 convolution_add_fusion.3
  152.4 4.3 %collective-permute-done.12 = f32[128,128]{1,0:T(8,128)S(1)} collective-permute-done((f32[128,128]{1,0:T(8,128)S(1)}, f32[128,128]{1,0:T(8,128)S(1)}, u32[]{:S(2)}, u32[]{:S(2)}) %collective-permute-start.12) | collective-permute-done | bytes 65568 | tf_op jit(solution)/shard_map/ppermute | solution.py:25
  156.8 0.4 fusion.33
  157.6 1.3 collective-permute-start.25
  159.7 2.6 %collective-permute-start.20 = (f32[128,128]{1,0:T(8,128)S(1)}, f32[128,128]{1,0:T(8,128)S(1)}, u32[]{:S(2)}, u32[]{:S(2)}) collective-permute-start(f32[128,128]{1,0:T(8,128)S(1)} %add.355), channel_id=1, source_target_pairs={{0,15},{1,0},{2,1},{3,2},{4,3},{5,4},{6,5},{7,6},{8,7},{9,8},{10,9... | collective-permute-start | bytes 196616 | tf_op jit(solution)/shard_map/ppermute | solution.py:25
  162.2 14.7 %all-reduce.9.cloned.1.call-done = (f32[128,128]{1,0:T(8,128)}, f32[128,128]{1,0:T(8,128)}) async-done(((f32[128,128]{1,0:T(8,128)}, f32[128,128]{1,0:T(8,128)}), (f32[128,128]{1,0:T(8,128)}, f32[128,128]{1,0:T(8,128)})) %all-reduce.9.cloned.1.call-update) | async-done | bytes 131088 | tf_op jit(solution)/shard_map/psum | solution.py:163
  176.9 0.7 collective-permute-start.14
  177.6 0.5 collective-permute-start.15
  178.1 0.4 convolution_add_fusion.2
  178.5 2.7 %collective-permute-done.14 = f32[128,128]{1,0:T(8,128)S(1)} collective-permute-done((f32[128,128]{1,0:T(8,128)S(1)}, f32[128,128]{1,0:T(8,128)S(1)}, u32[]{:S(2)}, u32[]{:S(2)}) %collective-permute-start.14) | collective-permute-done | bytes 65568 | tf_op jit(solution)/shard_map/ppermute | solution.py:25
  181.2 0.4 fusion.34
  182.1 0.7 collective-permute-start.26
  183.6 2.7 %collective-permute-start.21 = (f32[128,128]{1,0:T(8,128)S(1)}, f32[128,128]{1,0:T(8,128)S(1)}, u32[]{:S(2)}, u32[]{:S(2)}) collective-permute-start(f32[128,128]{1,0:T(8,128)S(1)} %add.356), channel_id=1, source_target_pairs={{0,15},{1,0},{2,1},{3,2},{4,3},{5,4},{6,5},{7,6},{8,7},{9,8},{10,9... | collective-permute-start | bytes 196616 | tf_op jit(solution)/shard_map/ppermute | solution.py:25
  186.2 1.0 collective-permute-start.16
  187.3 0.4 convolution_add_fusion.1
  187.7 3.1 %collective-permute-done.16 = f32[128,128]{1,0:T(8,128)S(1)} collective-permute-done((f32[128,128]{1,0:T(8,128)S(1)}, f32[128,128]{1,0:T(8,128)S(1)}, u32[]{:S(2)}, u32[]{:S(2)}) %collective-permute-start.16) | collective-permute-done | bytes 65568 | tf_op jit(solution)/shard_map/ppermute | solution.py:25
  190.9 0.4 fusion.35
  191.7 19.4 %all-reduce.11.cloned.1.call-done = (f32[128,128]{1,0:T(8,128)}, f32[128,128]{1,0:T(8,128)}) async-done(((f32[128,128]{1,0:T(8,128)}, f32[128,128]{1,0:T(8,128)}), (f32[128,128]{1,0:T(8,128)}, f32[128,128]{1,0:T(8,128)})) %all-reduce.11.cloned.1.call-update) | async-done | bytes 131088 | tf_op jit(solution)/shard_map/psum | solution.py:163
  211.2 1.5 collective-permute-start.27
  213.5 0.4 copy-done.4
  214.1 0.6 collective-permute-start.22
  214.7 0.4 fusion.2
  215.1 0.8 copy.78
  216.0 0.7 copy.80
  216.7 1.6 collective-permute-done.22
  218.5 0.7 copy.79
  (99 shorter events, 10.5 us)
Async XLA Ops:
  7.2 18.4 %copy-start = (f32[128,4,128]{2,1,0:T(4,128)S(1)}, f32[128,4,128]{2,1,0:T(4,128)}, u32[]{:S(2)}) copy-start(f32[128,4,128]{2,1,0:T(4,128)} %param.15) | copy-start | bytes 786436
  7.2 2.5 %copy-start.5 = (f32[128,64]{0,1:T(8,128)S(1)}, f32[128,64]{0,1:T(8,128)}, u32[]{:S(2)}) copy-start(f32[128,64]{0,1:T(8,128)} %param.17) | copy-start | bytes 98308
  7.2 109.5 %all-reduce.7.cloned.1.call-start = ((), (), s32[]{:S(2)}) async-start(), calls=%async_computation | async-start | bytes 262144 | tf_op jit(solution)/shard_map/psum | solution.py:19
  8.1 12.8 %collective-permute-start = (f32[128,64]{1,0:T(8,128)S(1)}, f32[128,64]{1,0:T(8,128)S(1)}, u32[]{:S(2)}, u32[]{:S(2)}) collective-permute-start(f32[128,64]{1,0:T(8,128)S(1)} %copy.10), channel_id=1, source_target_pairs={{0,16},{16,0},{1,17},{17,1},{2,18},{18,2},{3,19},{19,3},{4,20},{20... | collective-permute-start | bytes 98312 | tf_op jit(solution)/shard_map/ppermute | solution.py:14
  9.8 13.5 %collective-permute-start.5 = (f32[128,64]{1,0:T(8,128)S(1)}, f32[128,64]{1,0:T(8,128)S(1)}, u32[]{:S(2)}, u32[]{:S(2)}) collective-permute-start(f32[128,64]{1,0:T(8,128)S(1)} %copy.24), channel_id=1, source_target_pairs={{0,16},{16,0},{1,17},{17,1},{2,18},{18,2},{3,19},{19,3},{4,20},{20... | collective-permute-start | bytes 98312 | tf_op jit(solution)/shard_map/ppermute | solution.py:14
  10.4 0.7 copy-start.6
  10.4 10.4 %copy-start.1 = (f32[128,4,128]{2,1,0:T(4,128)S(1)}, f32[128,4,128]{2,1,0:T(4,128)}, u32[]{:S(2)}) copy-start(f32[128,4,128]{2,1,0:T(4,128)} %param.18) | copy-start | bytes 786436
  21.7 4.6 %collective-permute-start.1 = (f32[128,128]{1,0:T(8,128)S(1)}, f32[128,128]{1,0:T(8,128)S(1)}, u32[]{:S(2)}, u32[]{:S(2)}) collective-permute-start(f32[128,128]{1,0:T(8,128)S(1)} %get-tuple-element.82), channel_id=1, source_target_pairs={{0,1},{1,2},{2,3},{3,4},{4,5},{5,6},{6,7},{7,8},{8,9},{9,10},{10,1... | collective-permute-start | bytes 196616 | tf_op jit(solution)/shard_map/ppermute | solution.py:25
  24.0 94.0 %collective-permute-start.6 = (f32[128,128]{1,0:T(8,128)S(1)}, f32[128,128]{1,0:T(8,128)S(1)}, u32[]{:S(2)}, u32[]{:S(2)}) collective-permute-start(f32[128,128]{1,0:T(8,128)S(1)} %get-tuple-element.80), channel_id=1, source_target_pairs={{0,1},{1,2},{2,3},{3,4},{4,5},{5,6},{6,7},{7,8},{8,9},{9,10},{10,1... | collective-permute-start | bytes 196616 | tf_op jit(solution)/shard_map/ppermute | solution.py:25
  26.0 150.9 %all-reduce.9.cloned.1.call-start = ((), (), s32[]{:S(2)}) async-start(), calls=%async_computation.1 | async-start | bytes 262144 | tf_op jit(solution)/shard_map/psum | solution.py:163
  26.3 91.8 %collective-permute-start.2 = (f32[128,128]{1,0:T(8,128)S(1)}, f32[128,128]{1,0:T(8,128)S(1)}, u32[]{:S(2)}, u32[]{:S(2)}) collective-permute-start(f32[128,128]{1,0:T(8,128)S(1)} %collective-permute-done.1), channel_id=1, source_target_pairs={{0,1},{1,2},{2,3},{3,4},{4,5},{5,6},{6,7},{7,8},{8,9},{9,10},{10,1... | collective-permute-start | bytes 196616 | tf_op jit(solution)/shard_map/ppermute | solution.py:25
  118.0 4.3 %collective-permute-start.7 = (f32[128,128]{1,0:T(8,128)S(1)}, f32[128,128]{1,0:T(8,128)S(1)}, u32[]{:S(2)}, u32[]{:S(2)}) collective-permute-start(f32[128,128]{1,0:T(8,128)S(1)} %collective-permute-done.6), channel_id=1, source_target_pairs={{0,1},{1,2},{2,3},{3,4},{4,5},{5,6},{6,7},{7,8},{8,9},{9,10},{10,1... | collective-permute-start | bytes 196616 | tf_op jit(solution)/shard_map/ppermute | solution.py:25
  118.1 4.9 %collective-permute-start.3 = (f32[128,128]{1,0:T(8,128)S(1)}, f32[128,128]{1,0:T(8,128)S(1)}, u32[]{:S(2)}, u32[]{:S(2)}) collective-permute-start(f32[128,128]{1,0:T(8,128)S(1)} %collective-permute-done.2), channel_id=1, source_target_pairs={{0,1},{1,2},{2,3},{3,4},{4,5},{5,6},{6,7},{7,8},{8,9},{9,10},{10,1... | collective-permute-start | bytes 196616 | tf_op jit(solution)/shard_map/ppermute | solution.py:25
  122.3 4.3 %collective-permute-start.8 = (f32[128,128]{1,0:T(8,128)S(1)}, f32[128,128]{1,0:T(8,128)S(1)}, u32[]{:S(2)}, u32[]{:S(2)}) collective-permute-start(f32[128,128]{1,0:T(8,128)S(1)} %collective-permute-done.7), channel_id=1, source_target_pairs={{0,1},{1,2},{2,3},{3,4},{4,5},{5,6},{6,7},{7,8},{8,9},{9,10},{10,1... | collective-permute-start | bytes 196616 | tf_op jit(solution)/shard_map/ppermute | solution.py:25
  123.0 5.7 %collective-permute-start.4 = (f32[128,128]{1,0:T(8,128)S(1)}, f32[128,128]{1,0:T(8,128)S(1)}, u32[]{:S(2)}, u32[]{:S(2)}) collective-permute-start(f32[128,128]{1,0:T(8,128)S(1)} %collective-permute-done.3), channel_id=1, source_target_pairs={{0,1},{1,2},{2,3},{3,4},{4,5},{5,6},{6,7},{7,8},{8,9},{9,10},{10,1... | collective-permute-start | bytes 196616 | tf_op jit(solution)/shard_map/ppermute | solution.py:25
  126.6 7.3 %collective-permute-start.9 = (f32[128,128]{1,0:T(8,128)S(1)}, f32[128,128]{1,0:T(8,128)S(1)}, u32[]{:S(2)}, u32[]{:S(2)}) collective-permute-start(f32[128,128]{1,0:T(8,128)S(1)} %collective-permute-done.8), channel_id=1, source_target_pairs={{0,1},{1,2},{2,3},{3,4},{4,5},{5,6},{6,7},{7,8},{8,9},{9,10},{10,1... | collective-permute-start | bytes 196616 | tf_op jit(solution)/shard_map/ppermute | solution.py:25
  129.7 0.8 copy-start.3
  134.7 1.0 copy-start.2
  136.2 10.9 %collective-permute-start.23 = (f32[128,128]{1,0:T(8,128)S(1)}, f32[128,128]{1,0:T(8,128)S(1)}, u32[]{:S(2)}, u32[]{:S(2)}) collective-permute-start(f32[128,128]{1,0:T(8,128)S(1)} %convolution_bitcast_fusion.11), channel_id=1, source_target_pairs={{0,15},{1,0},{2,1},{3,2},{4,3},{5,4},{6,5},{7,6},{8,7},{9,8},{10,9... | collective-permute-start | bytes 196616 | tf_op jit(solution)/shard_map/ppermute | solution.py:25
  141.2 8.0 %collective-permute-start.18 = (f32[128,128]{1,0:T(8,128)S(1)}, f32[128,128]{1,0:T(8,128)S(1)}, u32[]{:S(2)}, u32[]{:S(2)}) collective-permute-start(f32[128,128]{1,0:T(8,128)S(1)} %fusion.54), channel_id=1, source_target_pairs={{0,15},{1,0},{2,1},{3,2},{4,3},{5,4},{6,5},{7,6},{8,7},{9,8},{10,9... | collective-permute-start | bytes 196616 | tf_op jit(solution)/shard_map/ppermute | solution.py:25
  142.3 68.7 %all-reduce.11.cloned.1.call-start = ((), (), s32[]{:S(2)}) async-start(), calls=%async_computation.2 | async-start | bytes 262144 | tf_op jit(solution)/shard_map/psum | solution.py:163
  142.4 4.3 %collective-permute-start.10 = (f32[128,128]{1,0:T(8,128)S(1)}, f32[128,128]{1,0:T(8,128)S(1)}, u32[]{:S(2)}, u32[]{:S(2)}) collective-permute-start(f32[128,128]{1,0:T(8,128)S(1)} %collective-permute-done.4), channel_id=1, source_target_pairs={{0,15},{1,0},{2,1},{3,2},{4,3},{5,4},{6,5},{7,6},{8,7},{9,8},{10,9... | collective-permute-start | bytes 196616 | tf_op jit(solution)/shard_map/ppermute | solution.py:25
  142.5 6.3 %collective-permute-start.11 = (f32[128,128]{1,0:T(8,128)S(1)}, f32[128,128]{1,0:T(8,128)S(1)}, u32[]{:S(2)}, u32[]{:S(2)}) collective-permute-start(f32[128,128]{1,0:T(8,128)S(1)} %collective-permute-done.9), channel_id=1, source_target_pairs={{0,15},{1,0},{2,1},{3,2},{4,3},{5,4},{6,5},{7,6},{8,7},{9,8},{10,9... | collective-permute-start | bytes 196616 | tf_op jit(solution)/shard_map/ppermute | solution.py:25
  147.5 10.1 %collective-permute-start.24 = (f32[128,128]{1,0:T(8,128)S(1)}, f32[128,128]{1,0:T(8,128)S(1)}, u32[]{:S(2)}, u32[]{:S(2)}) collective-permute-start(f32[128,128]{1,0:T(8,128)S(1)} %fusion.56), channel_id=1, source_target_pairs={{0,15},{1,0},{2,1},{3,2},{4,3},{5,4},{6,5},{7,6},{8,7},{9,8},{10,9... | collective-permute-start | bytes 196616 | tf_op jit(solution)/shard_map/ppermute | solution.py:25
  149.5 10.1 %collective-permute-start.19 = (f32[128,128]{1,0:T(8,128)S(1)}, f32[128,128]{1,0:T(8,128)S(1)}, u32[]{:S(2)}, u32[]{:S(2)}) collective-permute-start(f32[128,128]{1,0:T(8,128)S(1)} %fusion.55), channel_id=1, source_target_pairs={{0,15},{1,0},{2,1},{3,2},{4,3},{5,4},{6,5},{7,6},{8,7},{9,8},{10,9... | collective-permute-start | bytes 196616 | tf_op jit(solution)/shard_map/ppermute | solution.py:25
  151.9 4.9 %collective-permute-start.12 = (f32[128,128]{1,0:T(8,128)S(1)}, f32[128,128]{1,0:T(8,128)S(1)}, u32[]{:S(2)}, u32[]{:S(2)}) collective-permute-start(f32[128,128]{1,0:T(8,128)S(1)} %collective-permute-done.10), channel_id=1, source_target_pairs={{0,15},{1,0},{2,1},{3,2},{4,3},{5,4},{6,5},{7,6},{8,7},{9,8},{10,9... | collective-permute-start | bytes 196616 | tf_op jit(solution)/shard_map/ppermute | solution.py:25
  151.9 7.0 %collective-permute-start.13 = (f32[128,128]{1,0:T(8,128)S(1)}, f32[128,128]{1,0:T(8,128)S(1)}, u32[]{:S(2)}, u32[]{:S(2)}) collective-permute-start(f32[128,128]{1,0:T(8,128)S(1)} %collective-permute-done.11), channel_id=1, source_target_pairs={{0,15},{1,0},{2,1},{3,2},{4,3},{5,4},{6,5},{7,6},{8,7},{9,8},{10,9... | collective-permute-start | bytes 196616 | tf_op jit(solution)/shard_map/ppermute | solution.py:25
  157.6 24.4 %collective-permute-start.25 = (f32[128,128]{1,0:T(8,128)S(1)}, f32[128,128]{1,0:T(8,128)S(1)}, u32[]{:S(2)}, u32[]{:S(2)}) collective-permute-start(f32[128,128]{1,0:T(8,128)S(1)} %add.361), channel_id=1, source_target_pairs={{0,15},{1,0},{2,1},{3,2},{4,3},{5,4},{6,5},{7,6},{8,7},{9,8},{10,9... | collective-permute-start | bytes 196616 | tf_op jit(solution)/shard_map/ppermute | solution.py:25
  159.7 23.8 %collective-permute-start.20 = (f32[128,128]{1,0:T(8,128)S(1)}, f32[128,128]{1,0:T(8,128)S(1)}, u32[]{:S(2)}, u32[]{:S(2)}) collective-permute-start(f32[128,128]{1,0:T(8,128)S(1)} %add.355), channel_id=1, source_target_pairs={{0,15},{1,0},{2,1},{3,2},{4,3},{5,4},{6,5},{7,6},{8,7},{9,8},{10,9... | collective-permute-start | bytes 196616 | tf_op jit(solution)/shard_map/ppermute | solution.py:25
  176.9 4.3 %collective-permute-start.14 = (f32[128,128]{1,0:T(8,128)S(1)}, f32[128,128]{1,0:T(8,128)S(1)}, u32[]{:S(2)}, u32[]{:S(2)}) collective-permute-start(f32[128,128]{1,0:T(8,128)S(1)} %collective-permute-done.12), channel_id=1, source_target_pairs={{0,15},{1,0},{2,1},{3,2},{4,3},{5,4},{6,5},{7,6},{8,7},{9,8},{10,9... | collective-permute-start | bytes 196616 | tf_op jit(solution)/shard_map/ppermute | solution.py:25
  177.6 5.2 %collective-permute-start.15 = (f32[128,128]{1,0:T(8,128)S(1)}, f32[128,128]{1,0:T(8,128)S(1)}, u32[]{:S(2)}, u32[]{:S(2)}) collective-permute-start(f32[128,128]{1,0:T(8,128)S(1)} %collective-permute-done.13), channel_id=1, source_target_pairs={{0,15},{1,0},{2,1},{3,2},{4,3},{5,4},{6,5},{7,6},{8,7},{9,8},{10,9... | collective-permute-start | bytes 196616 | tf_op jit(solution)/shard_map/ppermute | solution.py:25
  182.1 29.0 %collective-permute-start.26 = (f32[128,128]{1,0:T(8,128)S(1)}, f32[128,128]{1,0:T(8,128)S(1)}, u32[]{:S(2)}, u32[]{:S(2)}) collective-permute-start(f32[128,128]{1,0:T(8,128)S(1)} %add.362), channel_id=1, source_target_pairs={{0,15},{1,0},{2,1},{3,2},{4,3},{5,4},{6,5},{7,6},{8,7},{9,8},{10,9... | collective-permute-start | bytes 196616 | tf_op jit(solution)/shard_map/ppermute | solution.py:25
  183.6 30.0 %collective-permute-start.21 = (f32[128,128]{1,0:T(8,128)S(1)}, f32[128,128]{1,0:T(8,128)S(1)}, u32[]{:S(2)}, u32[]{:S(2)}) collective-permute-start(f32[128,128]{1,0:T(8,128)S(1)} %add.356), channel_id=1, source_target_pairs={{0,15},{1,0},{2,1},{3,2},{4,3},{5,4},{6,5},{7,6},{8,7},{9,8},{10,9... | collective-permute-start | bytes 196616 | tf_op jit(solution)/shard_map/ppermute | solution.py:25
  186.2 4.6 %collective-permute-start.16 = (f32[128,128]{1,0:T(8,128)S(1)}, f32[128,128]{1,0:T(8,128)S(1)}, u32[]{:S(2)}, u32[]{:S(2)}) collective-permute-start(f32[128,128]{1,0:T(8,128)S(1)} %collective-permute-done.14), channel_id=1, source_target_pairs={{0,15},{1,0},{2,1},{3,2},{4,3},{5,4},{6,5},{7,6},{8,7},{9,8},{10,9... | collective-permute-start | bytes 196616 | tf_op jit(solution)/shard_map/ppermute | solution.py:25
  187.2 25.5 %collective-permute-start.17 = (f32[128,128]{1,0:T(8,128)S(1)}, f32[128,128]{1,0:T(8,128)S(1)}, u32[]{:S(2)}, u32[]{:S(2)}) collective-permute-start(f32[128,128]{1,0:T(8,128)S(1)} %collective-permute-done.15), channel_id=1, source_target_pairs={{0,15},{1,0},{2,1},{3,2},{4,3},{5,4},{6,5},{7,6},{8,7},{9,8},{10,9... | collective-permute-start | bytes 196616 | tf_op jit(solution)/shard_map/ppermute | solution.py:25
  211.2 4.8 %collective-permute-start.27 = (f32[128,64]{1,0:T(8,128)S(1)}, f32[128,64]{1,0:T(8,128)S(1)}, u32[]{:S(2)}, u32[]{:S(2)}) collective-permute-start(f32[128,64]{1,0:T(8,128)S(1)} %slice_select_fusion), channel_id=1, source_target_pairs={{0,16},{16,0},{1,17},{17,1},{2,18},{18,2},{3,19},{19,3},{4,20},{20... | collective-permute-start | bytes 98312 | tf_op jit(solution)/shard_map/ppermute | solution.py:14
  213.1 0.8 copy-start.4
  214.1 4.3 %collective-permute-start.22 = (f32[128,64]{1,0:T(8,128)S(1)}, f32[128,64]{1,0:T(8,128)S(1)}, u32[]{:S(2)}, u32[]{:S(2)}) collective-permute-start(f32[128,64]{1,0:T(8,128)S(1)} %slice_select_fusion.1), channel_id=1, source_target_pairs={{0,16},{16,0},{1,17},{17,1},{2,18},{18,2},{3,19},{19,3},{4,20},{20... | collective-permute-start | bytes 98312 | tf_op jit(solution)/shard_map/ppermute | solution.py:14
Sparse Core Ops, SparseCore 0:
  26.1 90.5 all-reduce.6
  142.4 34.4 all-reduce.8
  179.3 31.7 all-reduce.10
